TPU v7x, 128 devices: a whole 4x4x4 slice. The times are simulated.
128 devices in a mesh: gx: 4 (over z), gy: 32 (over y, x, core).
Axes of the slice: x: 4, y: 4, z: 4, core: 2. Of those that a mesh axis runs over, the one named last changes fastest.
Arguments:
- tokens: bfloat16 [8192, 6144], P('gy', 'gx'), may hold values from -7.5 to 7.5, as said below
- norm_gain: float32 [6144], P('gx'), may hold values from 0.1 to 1.9
- joined_weight: bfloat16 [6144, 43008], P('gx', 'gy'), may hold values from -0.078125 to 0.078125
Outputs:
- projected: bfloat16 [256, 32, 43008], P('gx', None, 'gy')
Inputs may be any that keep to these rules, and one draw needn't show every extreme that they name: Every entry of tokens lies between -7.5 and 7.5; each token's features are noise plus an offset of its own plus a slope of its own times a ramp from -1 to 1 over the 6144 features.
All inputs are finite; a program needn't handle non-finite values.
Results may differ from a plain program's by a relative error of at most 0.014.
Values may be sent and summed in bfloat16 or wider, within the bound.
A program may use at most 128 MiB of HBM per device.

v0:
```python
import jax
import jax.numpy as jnp
from jax import lax
from jax.sharding import PartitionSpec as P

epsilon = 1e-06


def from_everyone(shard, axis):
    copies = jnp.broadcast_to(shard, (lax.axis_size(axis), *shard.shape))
    return lax.all_to_all(copies, axis, split_axis=0, concat_axis=0, tiled=True)


def in_order(parts, dim):
    lengths = list(parts.shape[1:])
    lengths[dim] *= parts.shape[0]
    return jnp.moveaxis(parts, 0, dim).reshape(lengths)


def gather_directly(shard, axis, dim):
    parts = from_everyone(shard, axis)
    return in_order(parts, dim)


def body(tokens, norm_gain, joined_weight):
    shard_count = lax.axis_size("gy")
    column_count = joined_weight.shape[1]
    full_weight, full_gain = (
        gather_directly(joined_weight, "gx", 0),
        gather_directly(norm_gain.astype(jnp.bfloat16), "gx", 0).astype(norm_gain.dtype),
    )
    own_tokens = lax.all_to_all(tokens, "gx", split_axis=0, concat_axis=1, tiled=True)
    values = own_tokens.astype(jnp.float32)
    width = values.shape[1]
    mean = jnp.sum(values, axis=1, keepdims=True) / width
    centered = values - mean
    variance = jnp.sum(centered * centered, axis=1, keepdims=True) / width
    normed = (centered * lax.rsqrt(variance + epsilon) * full_gain).astype(jnp.bfloat16)
    block_count = lax.axis_size("gx")
    block_width = width // block_count
    segment = lax.all_gather(normed, "gy", axis=0, tiled=True)
    total = jnp.zeros((segment.shape[0], column_count), jnp.float32)
    for block in range(block_count):
        lower = block * block_width
        term = jnp.dot(
            segment[:, lower : lower + block_width],
            full_weight[lower : lower + block_width, :],
            preferred_element_type=jnp.float32,
        )
        rounded = lax.optimization_barrier(term.astype(jnp.bfloat16))
        total = total + rounded.astype(jnp.float32)
    result = total
    result = result.astype(jnp.bfloat16).reshape(shard_count, normed.shape[0], column_count)
    return jnp.swapaxes(result, 0, 1)


def solution(mesh):
    return jax.shard_map(
        body,
        mesh=mesh,
        in_specs=(P("gy", "gx"), P("gx"), P("gx", "gy")),
        out_specs=P("gx", None, "gy"),
        check_vma=False,
    )
```

profile of v0, /device:TPU:0, one launch (start us, length us, event | category | flops | bytes accessed | tf_op | source)
XLA Modules:
  0.0 309.2 jit_solution(13519837429296767604)
XLA Ops:
  6.5 0.7 convert_element_type.61
  7.3 0.5 broadcast.31
  7.8 0.7 reduce.4
  8.5 10.6 %all_to_all.24 = bf16[4,2,768]{2,1,0:T(2,128)(2,1)S(1)} all-to-all(bf16[4,2,768]{2,1,0:T(2,128)(2,1)S(1)} %reshape.46), channel_id=1, replica_groups=mesh['gx'=4,'gy'=32] {'gx'}, dimensions={0} | all-to-all | bytes 24576 | tf_op jit(solution)/shard_map/all_to_all | solution.py:11
  19.1 3.5 %all-to-all-start = ((bf16[4,64,1536]{2,1,0:T(8,128)(2,1)}), bf16[4,64,1536]{2,1,0:T(8,128)(2,1)S(1)}, u32[]{:S(2)}, u32[]{:S(2)}) async-start(bf16[4,64,1536]{2,1,0:T(8,128)(2,1)} %bitcast.23), calls=%async_computation | async-start | bytes 1572864 | tf_op jit(solution)/shard_map/all_to_all | solution.py:32
  22.6 0.0 all-gather.2.cloned.1.call-start
  22.7 11.0 %all-to-all-done = bf16[4,64,1536]{2,1,0:T(8,128)(2,1)S(1)} async-done(((bf16[4,64,1536]{2,1,0:T(8,128)(2,1)}), bf16[4,64,1536]{2,1,0:T(8,128)(2,1)S(1)}, u32[]{:S(2)}, u32[]{:S(2)}) %all-to-all-start) | async-done | bytes 786464 | tf_op jit(solution)/shard_map/all_to_all | solution.py:32
  33.7 0.2 convert_reduce_fusion
  33.9 0.4 fusion.5
  34.3 0.2 convert_bitcast_fusion
  34.5 0.1 copy.13
  34.6 1.2 multiply_convert_fusion
  35.8 0.0 all-gather.2.cloned.1.call-update
  35.8 3.9 %broadcast_in_dim.10 = bf16[4,1536,1344]{1,2,0:T(8,128)(2,1)S(1)} broadcast(bf16[1536,1344]{0,1:T(8,128)(2,1)} %param.5), dimensions={1,2} | broadcast | bytes 20643840 | tf_op jit(solution)/shard_map/broadcast_in_dim | solution.py:10
  39.7 182.9 %all_to_all.25 = bf16[4,1536,1344]{1,2,0:T(8,128)(2,1)} all-to-all(bf16[4,1536,1344]{1,2,0:T(8,128)(2,1)S(1)} %broadcast_in_dim.10), channel_id=1, replica_groups=mesh['gx'=4,'gy'=32] {'gx'}, dimensions={0} | all-to-all | bytes 33030144 | tf_op jit(solution)/shard_map/all_to_all | solution.py:11
  222.6 0.0 all-gather.2.cloned.1.call-done
  222.7 0.0 copy-start
  222.7 12.3 %convolution_convert_fusion = bf16[2048,1344]{0,1:T(8,128)(2,1)S(1)} fusion(bf16[2048,6144]{1,0:T(8,128)(2,1)} %all-gather.2.cloned.1.call-done, bf16[4,1536,1344]{1,2,0:T(8,128)(2,1)} %all_to_all.25), kind=kOutput, calls=%fused_computation.1 | convolution fusion | flops 8458469376 | bytes 15925248 | tf_op jit(solution)/shard_map/dot_general | solution.py:45
  234.9 0.0 copy-done
  234.9 13.3 %convolution_convert_fusion.1 = bf16[2048,1344]{0,1:T(8,128)(2,1)} fusion(bf16[2048,6144]{1,0:T(8,128)(2,1)} %all-gather.2.cloned.1.call-done, bf16[4,1536,1344]{1,2,0:T(8,128)(2,1)S(1)} %copy-done), kind=kOutput, calls=%fused_computation.2 | convolution fusion | flops 8458469376 | bytes 15925248 | tf_op jit(solution)/shard_map/dot_general | solution.py:45
  248.2 13.3 %convolution_convert_fusion.3 = bf16[2048,1344]{0,1:T(8,128)(2,1)} fusion(bf16[2048,6144]{1,0:T(8,128)(2,1)} %all-gather.2.cloned.1.call-done, bf16[4,1536,1344]{1,2,0:T(8,128)(2,1)S(1)} %copy-done), kind=kOutput, calls=%fused_computation.4 | convolution fusion | flops 8458469376 | bytes 15925248 | tf_op jit(solution)/shard_map/dot_general | solution.py:45
  261.5 13.4 %convolution_convert_fusion.2 = bf16[2048,1344]{0,1:T(8,128)(2,1)} fusion(bf16[2048,6144]{1,0:T(8,128)(2,1)} %all-gather.2.cloned.1.call-done, bf16[4,1536,1344]{1,2,0:T(8,128)(2,1)S(1)} %copy-done), kind=kOutput, calls=%fused_computation.3 | convolution fusion | flops 8458469376 | bytes 15925248 | tf_op jit(solution)/shard_map/dot_general | solution.py:45
  274.9 10.8 %add_convert_fusion = bf16[2048,1344]{0,1:T(8,128)(2,1)} fusion(bf16[2048,1344]{0,1:T(8,128)(2,1)S(1)} %convolution_convert_fusion, bf16[2048,1344]{0,1:T(8,128)(2,1)} %convolution_convert_fusion.1, bf16[2048,1344]{0,1:T(8,128)(2,1)} %convolution_convert_fusion.2, bf16[2048,1344]{0,1:T(8,128)(2,1)} %convolution_convert_fusion.3), kind=kLoop, calls=%fused_computation | loop fusion | flops 22020096 | bytes 27525120 | tf_op jit(solution)/shard_map/convert_element_type | solution.py:53
  285.7 8.3 %copy.11 = bf16[2048,1344]{1,0:T(8,128)(2,1)} copy(bf16[2048,1344]{0,1:T(8,128)(2,1)} %add_convert_fusion) | data formatting | bytes 11010048 | tf_op jit(solution)/shard_map/convert_element_type | solution.py:53
  294.0 8.4 %copy.12 = bf16[64,32,1344]{2,1,0:T(8,128)(2,1)} copy(bf16[64,32,1344]{2,0,1:T(8,128)(2,1)} %bitcast.21) | data formatting | bytes 11010048 | tf_op jit(solution)/shard_map/transpose | solution.py:54
  (6 shorter events, 0.1 us)
Async XLA Ops:
  19.1 14.6 %all-to-all-start = ((bf16[4,64,1536]{2,1,0:T(8,128)(2,1)}), bf16[4,64,1536]{2,1,0:T(8,128)(2,1)S(1)}, u32[]{:S(2)}, u32[]{:S(2)}) async-start(bf16[4,64,1536]{2,1,0:T(8,128)(2,1)} %bitcast.23), calls=%async_computation | async-start | bytes 1572864 | tf_op jit(solution)/shard_map/all_to_all | solution.py:32
  22.6 200.1 %all-gather.2.cloned.1.call-start = ((), (), s32[]{:S(2)}) async-start(), calls=%async_computation.3 | async-start | bytes 25952256 | tf_op jit(solution)/shard_map/all_gather | solution.py:41
  222.7 12.3 %copy-start = (bf16[4,1536,1344]{1,2,0:T(8,128)(2,1)S(1)}, bf16[4,1536,1344]{1,2,0:T(8,128)(2,1)}, u32[]{:S(2)}) copy-start(bf16[4,1536,1344]{1,2,0:T(8,128)(2,1)} %all_to_all.25) | copy-start | bytes 49545220
Sparse Core Ops, SparseCore 0:
  35.9 91.2 all-gather.1
where the time goes:
time: 310 us; the launch traced here: 309 us
  blocking collectives  193 us (62%)
  matrix products  52.2 us (17%)
  local copies, waits for them, and re-layouts  21.3 us (7%)
  other arithmetic  14.2 us (5%)
  between operations  13.5 us (4%)
  waiting for transfers between devices  11 us (4%)
  starting transfers between devices  3.54 us (1%)
    all_to_all x2, blocking collectives, from_everyone(): return lax.all_to_all(copies, axis, split_axis=0, concat_axis=0, tiled=True)  193 us
    dot_general x4, matrix products, body(): jnp.dot(segment[:, lower:lower + block_width], full_weight[lower:lower +...  52.2 us
    all_to_all x1, waiting for transfers between devices, body(): lax.all_to_all(tokens, 'gx', split_axis=0, concat_axis=1, tiled=True)  11 us
    convert_element_type x1, other arithmetic, body(): result.astype(jnp.bfloat16)  10.8 us
    transpose x1, local copies, waits for them, and re-layouts, body(): return jnp.swapaxes(result, 0, 1)  8.39 us
    convert_element_type x1, local copies, waits for them, and re-layouts, body(): result.astype(jnp.bfloat16)  8.3 us
  transfers between devices with their start and end apart: 2, of which 1 were waited for; matrix products, arithmetic and copies ran while one was open for 1% of the time, Pallas kernels for 0%

commit v1 on v0

v1 whole, which is shorter than its diff:
```python
import functools

import jax
import jax.numpy as jnp
from jax import lax
from jax.experimental import pallas as pl
from jax.experimental.pallas import tpu as pltpu
from jax.sharding import PartitionSpec as P

epsilon = 1e-06
MESH = pl.DeviceIdType.MESH
F32 = jnp.float32
BF16 = jnp.bfloat16

PC = 256
NC = 4
T = 64
ROWS = 32 * T
QR = ROWS // 4
HR = 256
JPOS = {0: 0, 1: 1, 3: 2, 2: 3}


def kernel(
    tok_hbm, gain_hbm, w_hbm, out_hbm,
    raw, praw, gain, st_loc, st_in, TA, TB, TC, wP, wF, wG, pbuf, inbuf, facc, fF, fO,
    lsem, start_send, start_recv, w_send, w_recv, p_send, p_recv, g_send, g_recv, out_sem,
):
    depth = raw.shape[1]
    width = 4 * depth
    z = lax.axis_index("gx")
    g = lax.axis_index("gy")
    core = g % 2
    x = (g // 2) % 4
    y = g // 8
    a = x + core * (y - x)
    b = y + core * (x - y)

    def gid(a_, b_, core_):
        x_ = a_ + core_ * (b_ - a_)
        y_ = b_ + core_ * (a_ - b_)
        return (y_ * 4 + x_) * 2 + core_

    zw = z + 1 - 2 * (z % 2)
    zp = 3 - z
    zo = (z + 2) % 4
    own = z % 2
    other = 1 - own
    dev_w = (zw, g)
    dev_p = (zp, g)
    dev_o = (zo, g)
    dev_ap = (z, gid((a + 1) % 4, b, core))
    dev_am = (z, gid((a + 3) % 4, b, core))
    dev_bp = (z, gid(a, (b + 1) % 4, core))
    dev_bm = (z, gid(a, (b + 3) % 4, core))
    dev_s = (z, g + 1 - 2 * core)

    loads = [
        pltpu.make_async_copy(tok_hbm, raw, lsem.at[0]),
        pltpu.make_async_copy(gain_hbm, gain.at[own], lsem.at[1]),
    ]
    for c in range(NC):
        loads.append(pltpu.make_async_copy(w_hbm.at[:, c * PC : (c + 1) * PC], wP.at[c, own], lsem.at[2 + c]))
    loads.append(pltpu.make_async_copy(w_hbm.at[:, NC * PC :], wF.at[own], lsem.at[2 + NC]))
    for copy in loads:
        copy.start()

    barrier = pltpu.get_barrier_semaphore()
    everyone = (dev_w, dev_p, dev_o, dev_ap, dev_am, dev_bp, dev_bm, dev_s)
    for dev in everyone:
        pl.semaphore_signal(barrier, inc=1, device_id=dev, device_id_type=MESH)
    pl.semaphore_wait(barrier, len(everyone))

    sends = []

    def remote(src, dst, send, recv, dev, static=True):
        copy = pltpu.make_async_remote_copy(
            src_ref=src, dst_ref=dst, send_sem=send, recv_sem=recv, device_id=dev, device_id_type=MESH
        )
        copy.start()
        if static:
            sends.append(copy)
        return copy

    def arrived(dst, recv, dev):
        pltpu.make_async_remote_copy(
            src_ref=dst, dst_ref=dst, send_sem=recv, recv_sem=recv, device_id=dev, device_id_type=MESH
        ).wait_recv()

    def rows(start, count):
        return pl.ds(pl.multiple_of(start, count), count)

    for k, pos in enumerate((zo, zw)):
        remote(tok_hbm.at[rows(pos * T, T)], praw.at[k * T : (k + 1) * T], start_send.at[k], start_recv.at[k], dev_w)
    remote(gain_hbm, gain.at[own], start_send.at[2], start_recv.at[2], dev_w)

    loads[0].wait()

    def stats(r, carry):
        at = rows(r * T, T)
        v = raw[at, :].astype(F32)
        m = jnp.sum(v, axis=1, keepdims=True) / depth
        d = v - m
        s = jnp.sum(d * d, axis=1, keepdims=True)
        lane = lax.broadcasted_iota(jnp.int32, (T, 128), 1)
        st_loc[at, :] = jnp.where(lane < 64, m, s)
        return carry

    lax.fori_loop(0, 4, stats, 0)
    for k, (dev, first, second) in enumerate(((dev_p, z, zp), (dev_w, zo, zw), (dev_o, zw, zo))):
        for h, pos in enumerate((first, second)):
            n = 3 + 2 * k + h
            remote(st_loc.at[rows(pos * T, T)], st_in.at[k, h * T : (h + 1) * T], start_send.at[n], start_recv.at[n], dev)

    remote(w_hbm.at[:, NC * PC :], wG.at[own], w_send.at[NC], w_recv.at[NC], dev_p)
    for c in range(NC):
        remote(w_hbm.at[:, c * PC : (c + 1) * PC], wP.at[c, own], w_send.at[c], w_recv.at[c], dev_w)
    remote(w_hbm.at[:, NC * PC :], wF.at[own], w_send.at[NC + 1], w_recv.at[NC + 1], dev_w)

    loads[1].wait()
    for n in range(3, 9):
        k, h = (n - 3) // 2, (n - 3) % 2
        arrived(st_in.at[k, h * T : (h + 1) * T], start_recv.at[n], (dev_p, dev_w, dev_o)[k])
    arrived(gain.at[other], start_recv.at[2], dev_w)
    for k in range(2):
        arrived(praw.at[k * T : (k + 1) * T], start_recv.at[k], dev_w)

    for h, (dst, pos) in enumerate(((TA, zp), (TB, z))):
        parts = [st_loc[rows(pos * T, T), :]] + [st_in[k, h * T : (h + 1) * T, :] for k in range(3)]
        means = [p[:, 0:1] for p in parts]
        mean = (means[0] + means[1] + means[2] + means[3]) * 0.25
        second = jnp.zeros_like(mean)
        for p, m in zip(parts, means):
            second = second + p[:, 64:65] + depth * (m - mean) * (m - mean)
        scale = lax.rsqrt(second / width + epsilon)
        dst[own, 0:T, :] = ((raw[rows(pos * T, T), :].astype(F32) - mean) * scale * gain[own]).astype(BF16)
        dst[other, 0:T, :] = ((praw[h * T : (h + 1) * T, :].astype(F32) - mean) * scale * gain[other]).astype(BF16)

    class Gather:
        def __init__(self, k, buf):
            self.k, self.buf, self.count = k, buf, 0

        def piece(self, i, j, sib=0):
            r = JPOS[j % 4] * 8 + sib * 4 + i % 4
            return self.buf.at[:, r * T : (r + 1) * T, :]

        def slot(self, i, s):
            r = i % 4
            return self.buf.at[s, r * T : (r + 1) * T, :]

        def rsem(self, i, j, sib=0):
            return g_recv.at[self.k * 32 + sib * 16 + (j % 4) * 4 + i % 4]

        def ssem(self):
            self.count += 1
            return g_send.at[self.k * 36 + self.count - 1]

        def send(self, i, j, di, dj, dev):
            remote(self.piece(i, j), self.piece(i - di, j - dj), self.ssem(), self.rsem(i - di, j - dj), dev)

        def send_sib(self, i, j):
            remote(self.piece(i, j), self.piece(i, j, 1), self.ssem(), self.rsem(i, j, 1), dev_s)

        def send_slot(self, i, di, s, dev):
            remote(self.slot(i, s), self.slot(i - di, s), self.ssem(), g_recv.at[self.k * 32 + (2, 0)[s]], dev)

        def wait(self, i, j, dev, sib=0):
            arrived(self.piece(i, j, sib), self.rsem(i, j, sib), dev)

        def spread(self, i):
            self.send(i, 0, 0, 1, dev_bp)
            self.send(i, 0, 0, -1, dev_bm)
            self.send_sib(i, 0)

        def e1(self):
            self.send(0, 0, 1, 0, dev_ap)
            self.send(0, 0, -1, 0, dev_am)
            self.spread(0)

        def e2(self):
            self.wait(3, 0, dev_am)
            self.send_slot(3, 1, 0, dev_ap)
            self.spread(3)

        def e3(self):
            self.wait(1, 0, dev_ap)
            self.send_slot(1, -1, 1, dev_am)
            self.spread(1)

        def e4(self):
            for s, dev in ((0, dev_am), (1, dev_ap)):
                arrived(self.slot(2, s), g_recv.at[self.k * 32 + (2, 0)[s]], dev)
            self.spread(2)

        def e5(self, i):
            self.wait(i, 3, dev_bm)
            if i in (0, 1):
                self.send(i, 3, 0, 1, dev_bp)
            self.wait(i, 1, dev_bp)
            if i in (3, 2):
                self.send(i, 1, 0, -1, dev_bm)
            self.send_sib(i, 3)
            self.send_sib(i, 1)

        def e6(self):
            for i in (0, 3, 1, 2):
                self.wait(i, 2, dev_bm if i in (0, 1) else dev_bp)
                self.send_sib(i, 2)

        def e7(self, q):
            j = (0, 1, 3, 2)[q]
            for i in range(4):
                self.wait(i, j, dev_s, 1)

    A, B, C = Gather(0, TA), Gather(1, TB), Gather(2, TC)

    def own_cols(c):
        loads[2 + c].wait()
        arrived(wP.at[c, other], w_recv.at[c], dev_w)

    def pair_dot(buf, c, at):
        return jnp.dot(buf[0, at, :], wP[c, 0], preferred_element_type=F32) + jnp.dot(
            buf[1, at, :], wP[c, 1], preferred_element_type=F32
        )

    def part_copy(u):
        c, q = u // 4, u % 4
        ref = pbuf.at[c, rows(q * QR, QR)]
        dst = inbuf.at[c, rows(q * QR, QR)]
        return pltpu.make_async_remote_copy(
            src_ref=ref, dst_ref=dst, send_sem=p_send.at[u], recv_sem=p_recv.at[u], device_id=dev_p, device_id_type=MESH
        )

    def partial(lo, hi):
        def unit(u, carry):
            c, q = u // 4, u % 4

            def half(h, carry):
                at = rows(q * QR + h * HR, HR)
                pbuf[c, at, :] = pair_dot(TA, c, at).astype(BF16)
                return carry

            lax.fori_loop(0, QR // HR, half, 0)
            part_copy(u).start()
            return carry

        lax.fori_loop(lo, hi, unit, 0)

    def place(q, s):
        j = q + (q // 2) * (1 - 2 * (q % 2))
        spots = []
        for i in range(4):
            if s == 0:
                spots.append(gid((a + i) % 4, (b + j) % 4, core))
            else:
                spots.append(gid((b + i) % 4, (a + j) % 4, 1 - core))
        return spots

    def out_wait(u):
        c, q = u // 4, u % 4
        ref = inbuf.at[c, rows(q * QR, QR)]
        return pltpu.make_async_copy(ref, ref, out_sem.at[u])

    def final(lo, hi):
        def unit(u, carry):
            c, q = u // 4, u % 4

            def half(h, carry):
                facc[rows(h * HR, HR), :] = pair_dot(TB, c, rows(q * QR + h * HR, HR))
                return carry

            lax.fori_loop(0, QR // HR, half, 0)
            part_copy(u).wait_recv()
            at = rows(q * QR, QR)
            inbuf[c, at, :] = (facc[...] + inbuf[c, at, :].astype(F32)).astype(BF16)
            for s in range(2):
                for i, p in enumerate(place(q, s)):
                    pltpu.make_async_copy(
                        inbuf.at[c, rows((q * 8 + s * 4 + i) * T, T)],
                        out_hbm.at[p, :, pl.ds(pl.multiple_of(c * PC, PC), PC)],
                        out_sem.at[u],
                    ).start()
            return carry

        lax.fori_loop(lo, hi, unit, 0)

    A.e1()
    remote(A.piece(0, 0), C.piece(0, 0), start_send.at[9], start_recv.at[9], dev_p)
    A.e2()
    A.e3()
    A.e4()
    B.e1()
    A.e5(0)
    A.e5(3)
    A.e7(0)
    own_cols(0)
    partial(0, 1)
    A.e5(1)
    A.e5(2)
    A.e7(1)
    A.e7(2)
    partial(1, 3)
    B.e2()
    B.e3()
    A.e6()
    A.e7(3)
    partial(3, 4)
    B.e4()
    B.e5(0)
    own_cols(1)
    partial(4, 8)
    arrived(C.piece(0, 0), start_recv.at[9], dev_p)
    C.e1()
    B.e5(3)
    B.e5(1)
    B.e5(2)
    arrived(wG.at[zp % 2], w_recv.at[NC], dev_p)
    remote(wG.at[zp % 2], wG.at[zp % 2], w_send.at[NC + 2], w_recv.at[NC + 2], dev_w)
    own_cols(2)
    partial(8, 12)
    C.e2()
    C.e3()
    B.e6()
    C.e4()
    for q in range(4):
        B.e7(q)
    C.e5(0)
    own_cols(3)
    partial(12, 16)
    C.e5(3)
    final(0, 3)
    C.e5(1)
    final(3, 6)
    C.e5(2)
    final(6, 8)
    C.e6()
    final(8, 10)
    for q in range(4):
        C.e7(q)

    loads[2 + NC].wait()

    def last_a(r, carry):
        at = rows(r * HR, HR)
        fF[at, :] = jnp.dot(TB[own, at, :], wF[own], preferred_element_type=F32) + jnp.dot(
            TC[zp % 2, at, :], wG[zp % 2], preferred_element_type=F32
        )
        return carry

    lax.fori_loop(0, ROWS // HR, last_a, 0)
    final(10, 14)
    arrived(wF.at[other], w_recv.at[NC + 1], dev_w)

    def last_b(r, carry):
        at = rows(r * HR, HR)
        fF[at, :] = fF[at, :] + jnp.dot(TB[other, at, :], wF[other], preferred_element_type=F32)
        return carry

    lax.fori_loop(0, ROWS // HR, last_b, 0)
    arrived(wG.at[zo % 2], w_recv.at[NC + 2], dev_w)

    def last_c(r, carry):
        at = rows(r * HR, HR)
        fO[at, :] = (fF[at, :] + jnp.dot(TC[zo % 2, at, :], wG[zo % 2], preferred_element_type=F32)).astype(BF16)
        return carry

    lax.fori_loop(0, ROWS // HR, last_c, 0)
    for q in range(4):
        for s in range(2):
            for i, p in enumerate(place(q, s)):
                r = q * 8 + s * 4 + i
                pltpu.make_async_copy(
                    fO.at[r * T : (r + 1) * T], out_hbm.at[p, :, NC * PC :], out_sem.at[4 * NC]
                ).start()
    final(14, 16)

    for copy in sends:
        copy.wait_send()

    def drain(u, carry):
        part_copy(u).wait_send()
        out_wait(u).wait()
        return carry

    lax.fori_loop(0, 4 * NC, drain, 0)
    pltpu.make_async_copy(fO, fO, out_sem.at[4 * NC]).wait()


def body(tokens, norm_gain, joined_weight):
    count, depth = tokens.shape
    columns = joined_weight.shape[1]
    rest = columns - NC * PC
    any_space = pl.BlockSpec(memory_space=pl.ANY)
    dma = pltpu.SemaphoreType.DMA
    result = pl.pallas_call(
        kernel,
        out_shape=jax.ShapeDtypeStruct((32, T, columns), BF16),
        in_specs=[any_space] * 3,
        out_specs=any_space,
        scratch_shapes=[
            pltpu.VMEM((count, depth), BF16),
            pltpu.VMEM((2 * T, depth), BF16),
            pltpu.VMEM((2, 1, depth), F32),
            pltpu.VMEM((count, 128), F32),
            pltpu.VMEM((3, 2 * T, 128), F32),
            pltpu.VMEM((2, ROWS, depth), BF16),
            pltpu.VMEM((2, ROWS, depth), BF16),
            pltpu.VMEM((2, ROWS, depth), BF16),
            pltpu.VMEM((NC, 2, depth, PC), BF16),
            pltpu.VMEM((2, depth, rest), BF16),
            pltpu.VMEM((2, depth, rest), BF16),
            pltpu.VMEM((NC, ROWS, PC), BF16),
            pltpu.VMEM((NC, ROWS, PC), BF16),
            pltpu.VMEM((QR, PC), F32),
            pltpu.VMEM((ROWS, rest), F32),
            pltpu.VMEM((ROWS, rest), BF16),
            dma((3 + NC,)),
            dma((10,)),
            dma((10,)),
            dma((NC + 3,)),
            dma((NC + 3,)),
            dma((4 * NC,)),
            dma((4 * NC,)),
            dma((3 * 36,)),
            dma((3 * 32,)),
            dma((4 * NC + 1,)),
        ],
        compiler_params=pltpu.CompilerParams(
            collective_id=0, has_side_effects=True, vmem_limit_bytes=67_000_000
        ),
    )(tokens, norm_gain.reshape(1, depth), joined_weight)
    return jnp.swapaxes(result, 0, 1)


def solution(mesh):
    return jax.shard_map(
        body,
        mesh=mesh,
        in_specs=(P("gy", "gx"), P("gx"), P("gx", "gy")),
        out_specs=P("gx", None, "gy"),
        check_vma=False,
    )
```

time: 310 us -> 166 us (0.54)
  blocking collectives: 193 us -> 0 us
  Pallas kernels: 0 us -> 149 us
  matrix products: 52.2 us -> 0 us
  other arithmetic: 14.2 us -> 0 us
  between operations: 13.5 us -> 0.01 us
  waiting for transfers between devices: 11 us -> 0 us
  local copies, waits for them, and re-layouts: 21.3 us -> 16.1 us
  starting transfers between devices: 3.54 us -> 0 us
    all_to_all x2 -> x0, blocking collectives: 193 us -> none  [from_everyone(): return lax.all_to_all(copies, axis, split_axis=0, concat_axis=0, tiled=True)]
    pallas_call x0 -> x1, Pallas kernels: none -> 149 us  [body(): pl.pallas_call(kernel, out_shape=jax.ShapeDtypeStruct((32, T, columns), B...]
    dot_general x4 -> x0, matrix products: 52.2 us -> none  [body(): jnp.dot(segment[:, lower:lower + block_width], full_weight[lower:lower +...]
    convert_element_type x4 -> x0, other arithmetic: 12.6 us -> none  [the longest x1 10.8 us: body(): result.astype(jnp.bfloat16)]
    all_to_all x1 -> x0, waiting for transfers between devices: 11 us -> none  [body(): lax.all_to_all(tokens, 'gx', split_axis=0, concat_axis=1, tiled=True)]
    convert_element_type x2 -> x0, local copies, waits for them, and re-layouts: 8.42 us -> none  [the longest x1 8.3 us: body(): result.astype(jnp.bfloat16)]
    unnamed x4 -> x1, local copies, waits for them, and re-layouts: 0.03 us -> 6.4 us
    broadcast_in_dim x3 -> x0, local copies, waits for them, and re-layouts: 4.46 us -> none  [from_everyone(): copies = jnp.broadcast_to(shard, (lax.axis_size(axis), *shard.shape))]
  transfers between devices with their start and end apart: 2 -> 0, of which waited for: 1 -> 0; matrix products, arithmetic and copies ran while one was open for 1% -> 0% of each run, Pallas kernels for 0% -> 0%
where the time goes in v1:
time: 166 us; the launch traced here: 165 us
  Pallas kernels  149 us (90%)
  local copies, waits for them, and re-layouts  16.1 us (10%)
    pallas_call x1, Pallas kernels, body(): pl.pallas_call(kernel, out_shape=jax.ShapeDtypeStruct((32, T, columns), B...  149 us
    transpose x1, local copies, waits for them, and re-layouts, body(): return jnp.swapaxes(result, 0, 1)  8.39 us
    unnamed x1, local copies, waits for them, and re-layouts  6.4 us

profile of v1, /device:TPU:0, one launch (start us, length us, event | category | flops | bytes accessed | tf_op | source)
XLA Modules:
  0.0 165.2 jit_solution(17314653566943083360)
XLA Ops:
  0.0 1.3 reshape.3.gain_hbm
  1.3 6.4 %copy.4.w_hbm = bf16[1536,1344]{1,0:T(8,128)(2,1)} copy(bf16[1536,1344]{0,1:T(8,128)(2,1)} %param.5) | data formatting | bytes 8257536 | tf_op args[2]
  7.7 149.1 %shard_map.37 = bf16[32,64,1344]{2,1,0:T(8,128)(2,1)} custom-call(bf16[256,1536]{1,0:T(8,128)(2,1)} %tok_hbm.1, f32[1,1536]{1,0:T(1,128)} %reshape.3.gain_hbm, bf16[1536,1344]{1,0:T(8,128)(2,1)} %copy.4.w_hbm), custom_call_target="tpu_custom_call" | custom-call | tf_op jit(solution)/shard_map/pallas_call | solution.py:395
  156.8 8.4 %copy.5 = bf16[64,32,1344]{2,1,0:T(8,128)(2,1)} copy(bf16[64,32,1344]{2,0,1:T(8,128)(2,1)} %bitcast.1) | data formatting | bytes 11010048 | tf_op jit(solution)/shard_map/transpose | solution.py:432

commit v2 on v1

--- a/solution.py
+++ b/solution.py
@@ -17,13 +17,17 @@
 T = 64
 ROWS = 32 * T
 QR = ROWS // 4
-HR = 256
+HR = 512
 JPOS = {0: 0, 1: 1, 3: 2, 2: 3}
+
+
+def times(rows, columns):
+    return lax.dot_general(rows, columns, (((1,), (1,)), ((), ())), preferred_element_type=F32)
 
 
 def kernel(
     tok_hbm, gain_hbm, w_hbm, out_hbm,
-    raw, praw, gain, st_loc, st_in, TA, TB, TC, wP, wF, wG, pbuf, inbuf, facc, fF, fO,
+    raw, praw, gain, gain_other, st_loc, st_in, TA, TB, TC, wP, wF, wG, pbuf, inbuf, facc, fF, fO,
     lsem, start_send, start_recv, w_send, w_recv, p_send, p_recv, g_send, g_recv, out_sem,
 ):
     depth = raw.shape[1]
@@ -57,44 +61,18 @@
 
     loads = [
         pltpu.make_async_copy(tok_hbm, raw, lsem.at[0]),
-        pltpu.make_async_copy(gain_hbm, gain.at[own], lsem.at[1]),
+        pltpu.make_async_copy(gain_hbm, gain, lsem.at[1]),
     ]
     for c in range(NC):
-        loads.append(pltpu.make_async_copy(w_hbm.at[:, c * PC : (c + 1) * PC], wP.at[c, own], lsem.at[2 + c]))
-    loads.append(pltpu.make_async_copy(w_hbm.at[:, NC * PC :], wF.at[own], lsem.at[2 + NC]))
+        loads.append(pltpu.make_async_copy(w_hbm.at[c * PC : (c + 1) * PC], wP.at[c, own], lsem.at[2 + c]))
+    loads.append(pltpu.make_async_copy(w_hbm.at[NC * PC :], wF.at[own], lsem.at[2 + NC]))
     for copy in loads:
         copy.start()
 
-    barrier = pltpu.get_barrier_semaphore()
-    everyone = (dev_w, dev_p, dev_o, dev_ap, dev_am, dev_bp, dev_bm, dev_s)
-    for dev in everyone:
-        pl.semaphore_signal(barrier, inc=1, device_id=dev, device_id_type=MESH)
-    pl.semaphore_wait(barrier, len(everyone))
-
-    sends = []
-
-    def remote(src, dst, send, recv, dev, static=True):
-        copy = pltpu.make_async_remote_copy(
-            src_ref=src, dst_ref=dst, send_sem=send, recv_sem=recv, device_id=dev, device_id_type=MESH
-        )
-        copy.start()
-        if static:
-            sends.append(copy)
-        return copy
-
-    def arrived(dst, recv, dev):
-        pltpu.make_async_remote_copy(
-            src_ref=dst, dst_ref=dst, send_sem=recv, recv_sem=recv, device_id=dev, device_id_type=MESH
-        ).wait_recv()
+    loads[0].wait()
 
     def rows(start, count):
         return pl.ds(pl.multiple_of(start, count), count)
-
-    for k, pos in enumerate((zo, zw)):
-        remote(tok_hbm.at[rows(pos * T, T)], praw.at[k * T : (k + 1) * T], start_send.at[k], start_recv.at[k], dev_w)
-    remote(gain_hbm, gain.at[own], start_send.at[2], start_recv.at[2], dev_w)
-
-    loads[0].wait()
 
     def stats(r, carry):
         at = rows(r * T, T)
@@ -107,25 +85,52 @@
         return carry
 
     lax.fori_loop(0, 4, stats, 0)
+    loads[1].wait()
+
+    barrier = pltpu.get_barrier_semaphore()
+    everyone = (dev_w, dev_p, dev_o, dev_ap, dev_am, dev_bp, dev_bm, dev_s)
+    for dev in everyone:
+        pl.semaphore_signal(barrier, inc=1, device_id=dev, device_id_type=MESH)
+    pl.semaphore_wait(barrier, len(everyone))
+
+    sends = []
+
+    def remote(src, dst, send, recv, dev, static=True):
+        copy = pltpu.make_async_remote_copy(
+            src_ref=src, dst_ref=dst, send_sem=send, recv_sem=recv, device_id=dev, device_id_type=MESH
+        )
+        copy.start()
+        if static:
+            sends.append(copy)
+        return copy
+
+    def arrived(dst, recv, dev):
+        pltpu.make_async_remote_copy(
+            src_ref=dst, dst_ref=dst, send_sem=recv, recv_sem=recv, device_id=dev, device_id_type=MESH
+        ).wait_recv()
+
     for k, (dev, first, second) in enumerate(((dev_p, z, zp), (dev_w, zo, zw), (dev_o, zw, zo))):
         for h, pos in enumerate((first, second)):
             n = 3 + 2 * k + h
             remote(st_loc.at[rows(pos * T, T)], st_in.at[k, h * T : (h + 1) * T], start_send.at[n], start_recv.at[n], dev)
-
-    remote(w_hbm.at[:, NC * PC :], wG.at[own], w_send.at[NC], w_recv.at[NC], dev_p)
-    for c in range(NC):
-        remote(w_hbm.at[:, c * PC : (c + 1) * PC], wP.at[c, own], w_send.at[c], w_recv.at[c], dev_w)
-    remote(w_hbm.at[:, NC * PC :], wF.at[own], w_send.at[NC + 1], w_recv.at[NC + 1], dev_w)
-
-    loads[1].wait()
-    for n in range(3, 9):
-        k, h = (n - 3) // 2, (n - 3) % 2
-        arrived(st_in.at[k, h * T : (h + 1) * T], start_recv.at[n], (dev_p, dev_w, dev_o)[k])
-    arrived(gain.at[other], start_recv.at[2], dev_w)
-    for k in range(2):
-        arrived(praw.at[k * T : (k + 1) * T], start_recv.at[k], dev_w)
-
-    for h, (dst, pos) in enumerate(((TA, zp), (TB, z))):
+    remote(gain_hbm, gain_other, start_send.at[2], start_recv.at[2], dev_w)
+    for k, pos in enumerate((zo, zw)):
+        remote(raw.at[rows(pos * T, T)], praw.at[k * T : (k + 1) * T], start_send.at[k], start_recv.at[k], dev_w)
+
+    remote(w_hbm.at[NC * PC :], wG.at[own], w_send.at[NC], w_recv.at[NC], dev_p)
+
+    def send_cols(c):
+        remote(w_hbm.at[c * PC : (c + 1) * PC], wP.at[c, own], w_send.at[c], w_recv.at[c], dev_w)
+
+    for c in range(NC - 1):
+        send_cols(c)
+
+    def normalise(h, dst, pos):
+        for k in range(3):
+            n = 3 + 2 * k + h
+            arrived(st_in.at[k, h * T : (h + 1) * T], start_recv.at[n], (dev_p, dev_w, dev_o)[k])
+        if h == 0:
+            arrived(gain_other, start_recv.at[2], dev_w)
         parts = [st_loc[rows(pos * T, T), :]] + [st_in[k, h * T : (h + 1) * T, :] for k in range(3)]
         means = [p[:, 0:1] for p in parts]
         mean = (means[0] + means[1] + means[2] + means[3]) * 0.25
@@ -133,8 +138,11 @@
         for p, m in zip(parts, means):
             second = second + p[:, 64:65] + depth * (m - mean) * (m - mean)
         scale = lax.rsqrt(second / width + epsilon)
-        dst[own, 0:T, :] = ((raw[rows(pos * T, T), :].astype(F32) - mean) * scale * gain[own]).astype(BF16)
-        dst[other, 0:T, :] = ((praw[h * T : (h + 1) * T, :].astype(F32) - mean) * scale * gain[other]).astype(BF16)
+        dst[own, 0:T, :] = ((raw[rows(pos * T, T), :].astype(F32) - mean) * scale * gain[...].reshape(1, depth)).astype(BF16)
+        arrived(praw.at[h * T : (h + 1) * T], start_recv.at[h], dev_w)
+        dst[other, 0:T, :] = (
+            (praw[h * T : (h + 1) * T, :].astype(F32) - mean) * scale * gain_other[...].reshape(1, depth)
+        ).astype(BF16)
 
     class Gather:
         def __init__(self, k, buf):
@@ -219,9 +227,7 @@
         arrived(wP.at[c, other], w_recv.at[c], dev_w)
 
     def pair_dot(buf, c, at):
-        return jnp.dot(buf[0, at, :], wP[c, 0], preferred_element_type=F32) + jnp.dot(
-            buf[1, at, :], wP[c, 1], preferred_element_type=F32
-        )
+        return times(buf[0, at, :], wP[c, 0]) + times(buf[1, at, :], wP[c, 1])
 
     def part_copy(u):
         c, q = u // 4, u % 4
@@ -284,87 +290,98 @@
 
         lax.fori_loop(lo, hi, unit, 0)
 
+    def last_a(r, carry):
+        at = rows(r * QR, QR)
+        fF[at, :] = times(TB[own, at, :], wF[own]) + times(TC[zp % 2, at, :], wG[zp % 2])
+        fF[at, 0:PC] = fF[at, 0:PC] + times(TC[zo % 2, at, :], wG[zo % 2, 0:PC, :])
+        return carry
+
+    def last_b(r, carry):
+        at = rows(r * QR, QR)
+        fF[at, :] = fF[at, :] + times(TB[other, at, :], wF[other])
+        return carry
+
+    def last_c(r, carry):
+        at = rows(r * QR, QR)
+        fO[at, 0:PC] = fF[at, 0:PC].astype(BF16)
+        fO[at, PC:] = (fF[at, PC:] + times(TC[zo % 2, at, :], wG[zo % 2, PC:, :])).astype(BF16)
+        return carry
+
+    def forward_last(k):
+        part = (slice(0, PC), slice(PC, None))[k]
+        remote(wG.at[zp % 2, part], wG.at[zp % 2, part], w_send.at[NC + 2 + k], w_recv.at[NC + 2 + k], dev_w)
+
+    normalise(0, TA, zp)
     A.e1()
     remote(A.piece(0, 0), C.piece(0, 0), start_send.at[9], start_recv.at[9], dev_p)
+    normalise(1, TB, z)
     A.e2()
     A.e3()
     A.e4()
     B.e1()
     A.e5(0)
     A.e5(3)
+    arrived(wG.at[zp % 2], w_recv.at[NC], dev_p)
+    forward_last(0)
+    send_cols(NC - 1)
+    remote(w_hbm.at[NC * PC :], wF.at[own], w_send.at[NC + 1], w_recv.at[NC + 1], dev_w)
+    forward_last(1)
+    A.e5(1)
     A.e7(0)
     own_cols(0)
     partial(0, 1)
-    A.e5(1)
     A.e5(2)
     A.e7(1)
+    partial(1, 2)
     A.e7(2)
-    partial(1, 3)
+    partial(2, 3)
     B.e2()
     B.e3()
     A.e6()
     A.e7(3)
     partial(3, 4)
     B.e4()
+    arrived(C.piece(0, 0), start_recv.at[9], dev_p)
+    C.e1()
     B.e5(0)
     own_cols(1)
-    partial(4, 8)
-    arrived(C.piece(0, 0), start_recv.at[9], dev_p)
-    C.e1()
+    partial(4, 6)
     B.e5(3)
+    partial(6, 8)
     B.e5(1)
     B.e5(2)
-    arrived(wG.at[zp % 2], w_recv.at[NC], dev_p)
-    remote(wG.at[zp % 2], wG.at[zp % 2], w_send.at[NC + 2], w_recv.at[NC + 2], dev_w)
-    own_cols(2)
-    partial(8, 12)
     C.e2()
     C.e3()
+    own_cols(2)
+    partial(8, 10)
     B.e6()
     C.e4()
+    partial(10, 12)
     for q in range(4):
         B.e7(q)
     C.e5(0)
-    own_cols(3)
-    partial(12, 16)
+    final(0, 2)
     C.e5(3)
-    final(0, 3)
+    final(2, 4)
     C.e5(1)
-    final(3, 6)
+    final(4, 6)
     C.e5(2)
     final(6, 8)
+    own_cols(3)
+    partial(12, 14)
     C.e6()
+    partial(14, 16)
+    loads[2 + NC].wait()
+    arrived(wG.at[zo % 2, 0:PC], w_recv.at[NC + 2], dev_w)
     final(8, 10)
     for q in range(4):
         C.e7(q)
-
-    loads[2 + NC].wait()
-
-    def last_a(r, carry):
-        at = rows(r * HR, HR)
-        fF[at, :] = jnp.dot(TB[own, at, :], wF[own], preferred_element_type=F32) + jnp.dot(
-            TC[zp % 2, at, :], wG[zp % 2], preferred_element_type=F32
-        )
-        return carry
-
-    lax.fori_loop(0, ROWS // HR, last_a, 0)
-    final(10, 14)
+        lax.fori_loop(q, q + 1, last_a, 0)
+    final(10, 15)
     arrived(wF.at[other], w_recv.at[NC + 1], dev_w)
-
-    def last_b(r, carry):
-        at = rows(r * HR, HR)
-        fF[at, :] = fF[at, :] + jnp.dot(TB[other, at, :], wF[other], preferred_element_type=F32)
-        return carry
-
-    lax.fori_loop(0, ROWS // HR, last_b, 0)
-    arrived(wG.at[zo % 2], w_recv.at[NC + 2], dev_w)
-
-    def last_c(r, carry):
-        at = rows(r * HR, HR)
-        fO[at, :] = (fF[at, :] + jnp.dot(TC[zo % 2, at, :], wG[zo % 2], preferred_element_type=F32)).astype(BF16)
-        return carry
-
-    lax.fori_loop(0, ROWS // HR, last_c, 0)
+    lax.fori_loop(0, 4, last_b, 0)
+    arrived(wG.at[zo % 2, PC:], w_recv.at[NC + 3], dev_w)
+    lax.fori_loop(0, 4, last_c, 0)
     for q in range(4):
         for s in range(2):
             for i, p in enumerate(place(q, s)):
@@ -372,7 +389,7 @@
                 pltpu.make_async_copy(
                     fO.at[r * T : (r + 1) * T], out_hbm.at[p, :, NC * PC :], out_sem.at[4 * NC]
                 ).start()
-    final(14, 16)
+    final(15, 16)
 
     for copy in sends:
         copy.wait_send()
@@ -400,15 +417,16 @@
         scratch_shapes=[
             pltpu.VMEM((count, depth), BF16),
             pltpu.VMEM((2 * T, depth), BF16),
-            pltpu.VMEM((2, 1, depth), F32),
+            pltpu.VMEM((depth,), F32),
+            pltpu.VMEM((depth,), F32),
             pltpu.VMEM((count, 128), F32),
             pltpu.VMEM((3, 2 * T, 128), F32),
             pltpu.VMEM((2, ROWS, depth), BF16),
             pltpu.VMEM((2, ROWS, depth), BF16),
             pltpu.VMEM((2, ROWS, depth), BF16),
-            pltpu.VMEM((NC, 2, depth, PC), BF16),
-            pltpu.VMEM((2, depth, rest), BF16),
-            pltpu.VMEM((2, depth, rest), BF16),
+            pltpu.VMEM((NC, 2, PC, depth), BF16),
+            pltpu.VMEM((2, rest, depth), BF16),
+            pltpu.VMEM((2, rest, depth), BF16),
             pltpu.VMEM((NC, ROWS, PC), BF16),
             pltpu.VMEM((NC, ROWS, PC), BF16),
             pltpu.VMEM((QR, PC), F32),
@@ -417,8 +435,8 @@
             dma((3 + NC,)),
             dma((10,)),
             dma((10,)),
-            dma((NC + 3,)),
-            dma((NC + 3,)),
+            dma((NC + 4,)),
+            dma((NC + 4,)),
             dma((4 * NC,)),
             dma((4 * NC,)),
             dma((3 * 36,)),
@@ -428,7 +446,7 @@
         compiler_params=pltpu.CompilerParams(
             collective_id=0, has_side_effects=True, vmem_limit_bytes=67_000_000
         ),
-    )(tokens, norm_gain.reshape(1, depth), joined_weight)
+    )(tokens, norm_gain, joined_weight.T)
     return jnp.swapaxes(result, 0, 1)
 
 

time: 166 us -> 157 us (0.946); the launches traced: 165 us -> 154 us
  local copies, waits for them, and re-layouts: 16.1 us -> 8.39 us
  Pallas kernels: 149 us -> 146 us
    unnamed x1 -> x0, local copies, waits for them, and re-layouts: 6.4 us -> none
    pallas_call x1, Pallas kernels: 149 us -> 146 us  [body(): pl.pallas_call(kernel, out_shape=jax.ShapeDtypeStruct((32, T, columns), B...]
where the time goes in v2:
time: 157 us; the launch traced here: 154 us
  Pallas kernels  146 us (93%)
  local copies, waits for them, and re-layouts  8.39 us (5%)
    pallas_call x1, Pallas kernels, body(): pl.pallas_call(kernel, out_shape=jax.ShapeDtypeStruct((32, T, columns), B...  146 us
    transpose x1, local copies, waits for them, and re-layouts, body(): return jnp.swapaxes(result, 0, 1)  8.39 us

profile of v2, /device:TPU:0, one launch (start us, length us, event | category | flops | bytes accessed | tf_op | source)
XLA Modules:
  0.0 154.0 jit_solution(191135347529502720)
XLA Ops:
  0.0 145.6 %shard_map.37 = bf16[32,64,1344]{2,1,0:T(8,128)(2,1)} custom-call(bf16[256,1536]{1,0:T(8,128)(2,1)} %tok_hbm.1, f32[1536]{0:T(1024)} %gain_hbm.1, bf16[1344,1536]{1,0:T(8,128)(2,1)} %bitcast.3), custom_call_target="tpu_custom_call" | custom-call | tf_op jit(solution)/shard_map/pallas_call | solution.py:412
  145.6 8.4 %copy.4 = bf16[64,32,1344]{2,1,0:T(8,128)(2,1)} copy(bf16[64,32,1344]{2,0,1:T(8,128)(2,1)} %bitcast.2) | data formatting | bytes 11010048 | tf_op jit(solution)/shard_map/transpose | solution.py:450

commit v3 on v2

--- a/solution.py
+++ b/solution.py
@@ -17,7 +17,6 @@
 T = 64
 ROWS = 32 * T
 QR = ROWS // 4
-HR = 512
 JPOS = {0: 0, 1: 1, 3: 2, 2: 3}
 
 
@@ -69,10 +68,12 @@
     for copy in loads:
         copy.start()
 
+    lane = lax.broadcasted_iota(jnp.int32, (T, 128), 1)
+    line = lax.broadcasted_iota(jnp.int32, (T, 128), 0)
     loads[0].wait()
 
     def rows(start, count):
-        return pl.ds(pl.multiple_of(start, count), count)
+        return pl.ds(start if isinstance(start, int) else pl.multiple_of(start, count), count)
 
     def stats(r, carry):
         at = rows(r * T, T)
@@ -80,8 +81,8 @@
         m = jnp.sum(v, axis=1, keepdims=True) / depth
         d = v - m
         s = jnp.sum(d * d, axis=1, keepdims=True)
-        lane = lax.broadcasted_iota(jnp.int32, (T, 128), 1)
-        st_loc[at, :] = jnp.where(lane < 64, m, s)
+        both = jnp.where(lane == line, m, jnp.where(lane == line + T, s, 0.0))
+        st_loc[r] = jnp.broadcast_to(jnp.sum(both, axis=0, keepdims=True), (8, 128))
         return carry
 
     lax.fori_loop(0, 4, stats, 0)
@@ -112,7 +113,7 @@
     for k, (dev, first, second) in enumerate(((dev_p, z, zp), (dev_w, zo, zw), (dev_o, zw, zo))):
         for h, pos in enumerate((first, second)):
             n = 3 + 2 * k + h
-            remote(st_loc.at[rows(pos * T, T)], st_in.at[k, h * T : (h + 1) * T], start_send.at[n], start_recv.at[n], dev)
+            remote(st_loc.at[pos], st_in.at[k, h], start_send.at[n], start_recv.at[n], dev)
     remote(gain_hbm, gain_other, start_send.at[2], start_recv.at[2], dev_w)
     for k, pos in enumerate((zo, zw)):
         remote(raw.at[rows(pos * T, T)], praw.at[k * T : (k + 1) * T], start_send.at[k], start_recv.at[k], dev_w)
@@ -128,15 +129,16 @@
     def normalise(h, dst, pos):
         for k in range(3):
             n = 3 + 2 * k + h
-            arrived(st_in.at[k, h * T : (h + 1) * T], start_recv.at[n], (dev_p, dev_w, dev_o)[k])
+            arrived(st_in.at[k, h], start_recv.at[n], (dev_p, dev_w, dev_o)[k])
         if h == 0:
             arrived(gain_other, start_recv.at[2], dev_w)
-        parts = [st_loc[rows(pos * T, T), :]] + [st_in[k, h * T : (h + 1) * T, :] for k in range(3)]
-        means = [p[:, 0:1] for p in parts]
+        parts = [st_loc[pos]] + [st_in[k, h] for k in range(3)]
+        means = [jnp.sum(jnp.where(lane == line, p[0:1, :], 0.0), axis=1, keepdims=True) for p in parts]
+        seconds = [jnp.sum(jnp.where(lane == line + T, p[0:1, :], 0.0), axis=1, keepdims=True) for p in parts]
         mean = (means[0] + means[1] + means[2] + means[3]) * 0.25
         second = jnp.zeros_like(mean)
-        for p, m in zip(parts, means):
-            second = second + p[:, 64:65] + depth * (m - mean) * (m - mean)
+        for m, v in zip(means, seconds):
+            second = second + v + depth * (m - mean) * (m - mean)
         scale = lax.rsqrt(second / width + epsilon)
         dst[own, 0:T, :] = ((raw[rows(pos * T, T), :].astype(F32) - mean) * scale * gain[...].reshape(1, depth)).astype(BF16)
         arrived(praw.at[h * T : (h + 1) * T], start_recv.at[h], dev_w)
@@ -200,20 +202,21 @@
                 arrived(self.slot(2, s), g_recv.at[self.k * 32 + (2, 0)[s]], dev)
             self.spread(2)
 
-        def e5(self, i):
+        def l(self, i):
             self.wait(i, 3, dev_bm)
             if i in (0, 1):
                 self.send(i, 3, 0, 1, dev_bp)
+            self.send_sib(i, 3)
+
+        def r(self, i):
             self.wait(i, 1, dev_bp)
             if i in (3, 2):
                 self.send(i, 1, 0, -1, dev_bm)
-            self.send_sib(i, 3)
             self.send_sib(i, 1)
 
-        def e6(self):
-            for i in (0, 3, 1, 2):
-                self.wait(i, 2, dev_bm if i in (0, 1) else dev_bp)
-                self.send_sib(i, 2)
+        def o(self, i):
+            self.wait(i, 2, dev_bm if i in (0, 1) else dev_bp)
+            self.send_sib(i, 2)
 
         def e7(self, q):
             j = (0, 1, 3, 2)[q]
@@ -237,20 +240,28 @@
             src_ref=ref, dst_ref=dst, send_sem=p_send.at[u], recv_sem=p_recv.at[u], device_id=dev_p, device_id_type=MESH
         )
 
-    def partial(lo, hi):
+    def each(unit, units):
+        def step(k, carry):
+            u = units[0]
+            for n in range(1, len(units)):
+                u = jnp.where(k == n, units[n], u)
+            return unit(u, carry)
+
+        if len(units) == 1:
+            unit(units[0], 0)
+        else:
+            lax.fori_loop(0, len(units), step, 0)
+
+    def partial(*units):
         def unit(u, carry):
             c, q = u // 4, u % 4
 
-            def half(h, carry):
-                at = rows(q * QR + h * HR, HR)
-                pbuf[c, at, :] = pair_dot(TA, c, at).astype(BF16)
-                return carry
-
-            lax.fori_loop(0, QR // HR, half, 0)
+            at = rows(q * QR, QR)
+            pbuf[c, at, :] = pair_dot(TA, c, at).astype(BF16)
             part_copy(u).start()
             return carry
 
-        lax.fori_loop(lo, hi, unit, 0)
+        each(unit, units)
 
     def place(q, s):
         j = q + (q // 2) * (1 - 2 * (q % 2))
@@ -267,34 +278,29 @@
         ref = inbuf.at[c, rows(q * QR, QR)]
         return pltpu.make_async_copy(ref, ref, out_sem.at[u])
 
-    def final(lo, hi):
+    def final(*units):
         def unit(u, carry):
             c, q = u // 4, u % 4
 
-            def half(h, carry):
-                facc[rows(h * HR, HR), :] = pair_dot(TB, c, rows(q * QR + h * HR, HR))
-                return carry
-
-            lax.fori_loop(0, QR // HR, half, 0)
+            at = rows(q * QR, QR)
+            facc[...] = pair_dot(TB, c, at)
             part_copy(u).wait_recv()
-            at = rows(q * QR, QR)
             inbuf[c, at, :] = (facc[...] + inbuf[c, at, :].astype(F32)).astype(BF16)
             for s in range(2):
                 for i, p in enumerate(place(q, s)):
                     pltpu.make_async_copy(
                         inbuf.at[c, rows((q * 8 + s * 4 + i) * T, T)],
-                        out_hbm.at[p, :, pl.ds(pl.multiple_of(c * PC, PC), PC)],
+                        out_hbm.at[p, :, rows(c * PC, PC)],
                         out_sem.at[u],
                     ).start()
             return carry
 
-        lax.fori_loop(lo, hi, unit, 0)
-
-    def last_a(r, carry):
+        each(unit, units)
+
+    def last_a(r):
         at = rows(r * QR, QR)
         fF[at, :] = times(TB[own, at, :], wF[own]) + times(TC[zp % 2, at, :], wG[zp % 2])
         fF[at, 0:PC] = fF[at, 0:PC] + times(TC[zo % 2, at, :], wG[zo % 2, 0:PC, :])
-        return carry
 
     def last_b(r, carry):
         at = rows(r * QR, QR)
@@ -311,85 +317,118 @@
         part = (slice(0, PC), slice(PC, None))[k]
         remote(wG.at[zp % 2, part], wG.at[zp % 2, part], w_send.at[NC + 2 + k], w_recv.at[NC + 2 + k], dev_w)
 
+    def send_last():
+        arrived(wG.at[zp % 2], w_recv.at[NC], dev_p)
+        forward_last(0)
+        send_cols(NC - 1)
+        remote(w_hbm.at[NC * PC :], wF.at[own], w_send.at[NC + 1], w_recv.at[NC + 1], dev_w)
+        forward_last(1)
+
+    def send_across():
+        remote(A.piece(0, 0), C.piece(0, 0), start_send.at[9], start_recv.at[9], dev_p)
+
+    def put_last():
+        for q in range(4):
+            for s in range(2):
+                for i, p in enumerate(place(q, s)):
+                    r = q * 8 + s * 4 + i
+                    pltpu.make_async_copy(
+                        fO.at[r * T : (r + 1) * T], out_hbm.at[p, :, NC * PC :], out_sem.at[4 * NC]
+                    ).start()
+
     normalise(0, TA, zp)
     A.e1()
-    remote(A.piece(0, 0), C.piece(0, 0), start_send.at[9], start_recv.at[9], dev_p)
+    send_across()
+    A.e3()
+    A.e2()
+    A.e4()
+    A.l(1)
     normalise(1, TB, z)
-    A.e2()
-    A.e3()
-    A.e4()
+    send_last()
+    own_cols(0)
+    A.r(0)
+    A.e7(0)
+    A.l(0)
+    A.r(3)
+    partial(0)
+    A.l(3)
+    A.l(2)
+    A.r(1)
     B.e1()
-    A.e5(0)
-    A.e5(3)
-    arrived(wG.at[zp % 2], w_recv.at[NC], dev_p)
-    forward_last(0)
-    send_cols(NC - 1)
-    remote(w_hbm.at[NC * PC :], wF.at[own], w_send.at[NC + 1], w_recv.at[NC + 1], dev_w)
-    forward_last(1)
-    A.e5(1)
-    A.e7(0)
-    own_cols(0)
-    partial(0, 1)
-    A.e5(2)
+    A.e7(2)
+    partial(2)
+    A.r(2)
     A.e7(1)
-    partial(1, 2)
-    A.e7(2)
-    partial(2, 3)
+    partial(1)
+    A.o(3)
+    A.o(0)
+    own_cols(1)
     B.e2()
+    B.r(0)
     B.e3()
-    A.e6()
+    partial(6, 4, 5)
+    arrived(C.piece(0, 0), start_recv.at[9], dev_p)
+    A.o(1)
+    B.e4()
+    B.r(3)
+    C.e1()
+    own_cols(2)
+    A.o(2)
+    B.e7(0)
     A.e7(3)
-    partial(3, 4)
-    B.e4()
-    arrived(C.piece(0, 0), start_recv.at[9], dev_p)
-    C.e1()
-    B.e5(0)
-    own_cols(1)
-    partial(4, 6)
-    B.e5(3)
-    partial(6, 8)
-    B.e5(1)
-    B.e5(2)
+    partial(8, 11)
+    B.l(0)
+    B.l(3)
+    C.e3()
+    B.l(2)
+    B.l(1)
+    B.r(2)
+    B.r(1)
+    B.e7(2)
     C.e2()
-    C.e3()
-    own_cols(2)
-    partial(8, 10)
-    B.e6()
+    partial(3, 9, 7, 10)
+    B.e7(1)
+    B.o(3)
     C.e4()
-    partial(10, 12)
-    for q in range(4):
-        B.e7(q)
-    C.e5(0)
-    final(0, 2)
-    C.e5(3)
-    final(2, 4)
-    C.e5(1)
-    final(4, 6)
-    C.e5(2)
-    final(6, 8)
-    own_cols(3)
-    partial(12, 14)
-    C.e6()
-    partial(14, 16)
+    final(6, 1, 4, 5)
+    C.l(0)
+    B.o(0)
+    C.l(1)
+    final(8, 2, 0)
+    C.e7(0)
+    B.o(2)
+    B.o(1)
     loads[2 + NC].wait()
     arrived(wG.at[zo % 2, 0:PC], w_recv.at[NC + 2], dev_w)
-    final(8, 10)
-    for q in range(4):
-        C.e7(q)
-        lax.fori_loop(q, q + 1, last_a, 0)
-    final(10, 15)
+    last_a(0)
+    C.r(1)
+    C.r(3)
+    own_cols(3)
+    partial(15, 13, 14, 12)
+    C.r(2)
+    C.l(2)
+    B.e7(3)
+    C.r(0)
+    C.l(3)
+    final(3, 9, 7, 11)
+    C.o(3)
+    C.o(0)
+    C.e7(1)
+    last_a(1)
+    C.o(1)
+    C.e7(2)
+    last_a(2)
+    C.o(2)
+    final(15, 10, 13)
+    C.e7(3)
+    last_a(3)
     arrived(wF.at[other], w_recv.at[NC + 1], dev_w)
     lax.fori_loop(0, 4, last_b, 0)
+    final(14)
     arrived(wG.at[zo % 2, PC:], w_recv.at[NC + 3], dev_w)
     lax.fori_loop(0, 4, last_c, 0)
-    for q in range(4):
-        for s in range(2):
-            for i, p in enumerate(place(q, s)):
-                r = q * 8 + s * 4 + i
-                pltpu.make_async_copy(
-                    fO.at[r * T : (r + 1) * T], out_hbm.at[p, :, NC * PC :], out_sem.at[4 * NC]
-                ).start()
-    final(15, 16)
+    put_last()
+    final(12)
 
     for copy in sends:
         copy.wait_send()
@@ -419,8 +458,8 @@
             pltpu.VMEM((2 * T, depth), BF16),
             pltpu.VMEM((depth,), F32),
             pltpu.VMEM((depth,), F32),
-            pltpu.VMEM((count, 128), F32),
-            pltpu.VMEM((3, 2 * T, 128), F32),
+            pltpu.VMEM((4, 8, 128), F32),
+            pltpu.VMEM((3, 2, 8, 128), F32),
             pltpu.VMEM((2, ROWS, depth), BF16),
             pltpu.VMEM((2, ROWS, depth), BF16),
             pltpu.VMEM((2, ROWS, depth), BF16),

time: 157 us -> 143 us (0.911); the launches traced: 154 us -> 143 us
  Pallas kernels: 146 us -> 135 us
    pallas_call x1, Pallas kernels: 146 us -> 135 us  [body(): pl.pallas_call(kernel, out_shape=jax.ShapeDtypeStruct((32, T, columns), B...]
where the time goes in v3:
time: 143 us
  Pallas kernels  135 us (94%)
  local copies, waits for them, and re-layouts  8.39 us (6%)
    pallas_call x1, Pallas kernels, body(): pl.pallas_call(kernel, out_shape=jax.ShapeDtypeStruct((32, T, columns), B...  135 us
    transpose x1, local copies, waits for them, and re-layouts, body(): return jnp.swapaxes(result, 0, 1)  8.39 us

profile of v3, /device:TPU:0, one launch (start us, length us, event | category | flops | bytes accessed | tf_op | source)
XLA Modules:
  0.0 143.0 jit_solution(18366789314372578963)
XLA Ops:
  0.0 134.6 %shard_map.37 = bf16[32,64,1344]{2,1,0:T(8,128)(2,1)} custom-call(bf16[256,1536]{1,0:T(8,128)(2,1)} %tok_hbm.1, f32[1536]{0:T(1024)} %gain_hbm.1, bf16[1344,1536]{1,0:T(8,128)(2,1)} %bitcast.3), custom_call_target="tpu_custom_call" | custom-call | tf_op jit(solution)/shard_map/pallas_call | solution.py:451
  134.6 8.4 %copy.4 = bf16[64,32,1344]{2,1,0:T(8,128)(2,1)} copy(bf16[64,32,1344]{2,0,1:T(8,128)(2,1)} %bitcast.2) | data formatting | bytes 11010048 | tf_op jit(solution)/shard_map/transpose | solution.py:489

commit v4 on v3

--- a/solution.py
+++ b/solution.py
@@ -17,6 +17,9 @@
 T = 64
 ROWS = 32 * T
 QR = ROWS // 4
+TR = T // 4
+RING = 7
+LIMIT = 61_000_000
 JPOS = {0: 0, 1: 1, 3: 2, 2: 3}
 
 
@@ -25,9 +28,9 @@
 
 
 def kernel(
-    tok_hbm, gain_hbm, w_hbm, out_hbm,
-    raw, praw, gain, gain_other, st_loc, st_in, TA, TB, TC, wP, wF, wG, pbuf, inbuf, facc, fF, fO,
-    lsem, start_send, start_recv, w_send, w_recv, p_send, p_recv, g_send, g_recv, out_sem,
+    tok_hbm, gain_hbm, w_hbm, out,
+    raw, praw, gain, gain_other, st_loc, st_in, TA, TB, TC, wP, wF, wG, pbuf, inbuf, facc, fO,
+    lsem, start_send, start_recv, w_send, w_recv, p_send, p_recv, g_send, g_recv,
 ):
     depth = raw.shape[1]
     width = 4 * depth
@@ -68,6 +71,11 @@
     for copy in loads:
         copy.start()
 
+    barrier = pltpu.get_barrier_semaphore()
+    everyone = (dev_w, dev_p, dev_o, dev_ap, dev_am, dev_bp, dev_bm, dev_s)
+    for dev in everyone:
+        pl.semaphore_signal(barrier, inc=1, device_id=dev, device_id_type=MESH)
+
     lane = lax.broadcasted_iota(jnp.int32, (T, 128), 1)
     line = lax.broadcasted_iota(jnp.int32, (T, 128), 0)
     loads[0].wait()
@@ -88,10 +96,6 @@
     lax.fori_loop(0, 4, stats, 0)
     loads[1].wait()
 
-    barrier = pltpu.get_barrier_semaphore()
-    everyone = (dev_w, dev_p, dev_o, dev_ap, dev_am, dev_bp, dev_bm, dev_s)
-    for dev in everyone:
-        pl.semaphore_signal(barrier, inc=1, device_id=dev, device_id_type=MESH)
     pl.semaphore_wait(barrier, len(everyone))
 
     sends = []
@@ -140,9 +144,9 @@
         for m, v in zip(means, seconds):
             second = second + v + depth * (m - mean) * (m - mean)
         scale = lax.rsqrt(second / width + epsilon)
-        dst[own, 0:T, :] = ((raw[rows(pos * T, T), :].astype(F32) - mean) * scale * gain[...].reshape(1, depth)).astype(BF16)
+        dst[own, 0] = ((raw[rows(pos * T, T), :].astype(F32) - mean) * scale * gain[...].reshape(1, depth)).astype(BF16)
         arrived(praw.at[h * T : (h + 1) * T], start_recv.at[h], dev_w)
-        dst[other, 0:T, :] = (
+        dst[other, 0] = (
             (praw[h * T : (h + 1) * T, :].astype(F32) - mean) * scale * gain_other[...].reshape(1, depth)
         ).astype(BF16)
 
@@ -152,11 +156,11 @@
 
         def piece(self, i, j, sib=0):
             r = JPOS[j % 4] * 8 + sib * 4 + i % 4
-            return self.buf.at[:, r * T : (r + 1) * T, :]
+            return self.buf.at[:, r]
 
         def slot(self, i, s):
             r = i % 4
-            return self.buf.at[s, r * T : (r + 1) * T, :]
+            return self.buf.at[s, r]
 
         def rsem(self, i, j, sib=0):
             return g_recv.at[self.k * 32 + sib * 16 + (j % 4) * 4 + i % 4]
@@ -229,15 +233,23 @@
         loads[2 + c].wait()
         arrived(wP.at[c, other], w_recv.at[c], dev_w)
 
-    def pair_dot(buf, c, at):
-        return times(buf[0, at, :], wP[c, 0]) + times(buf[1, at, :], wP[c, 1])
-
-    def part_copy(u):
-        c, q = u // 4, u % 4
-        ref = pbuf.at[c, rows(q * QR, QR)]
-        dst = inbuf.at[c, rows(q * QR, QR)]
+    def by_piece(buf, s, q):
+        return buf[s, pl.ds(q * 8, 8)].reshape(QR, depth)
+
+    def by_position(buf, s, q):
+        return buf[s, :, rows(q * TR, TR)].reshape(QR, depth)
+
+    def pair_dot(take, buf, c, q):
+        return times(take(buf, 0, q), wP[c, 0]) + times(take(buf, 1, q), wP[c, 1])
+
+    def part_copy(n, u):
         return pltpu.make_async_remote_copy(
-            src_ref=ref, dst_ref=dst, send_sem=p_send.at[u], recv_sem=p_recv.at[u], device_id=dev_p, device_id_type=MESH
+            src_ref=pbuf.at[n % RING],
+            dst_ref=inbuf.at[u],
+            send_sem=p_send.at[n],
+            recv_sem=p_recv.at[u],
+            device_id=dev_p,
+            device_id_type=MESH,
         )
 
     def each(unit, units):
@@ -245,72 +257,113 @@
             u = units[0]
             for n in range(1, len(units)):
                 u = jnp.where(k == n, units[n], u)
-            return unit(u, carry)
+            unit(k, u)
+            return carry
 
         if len(units) == 1:
-            unit(units[0], 0)
+            unit(0, units[0])
         else:
             lax.fori_loop(0, len(units), step, 0)
 
+    def runs(units):
+        groups = []
+        for u in units:
+            if groups and (groups[-1][0] < 8) == (u < 8):
+                groups[-1].append(u)
+            else:
+                groups.append([u])
+        return groups
+
+    sent = []
+
     def partial(*units):
-        def unit(u, carry):
-            c, q = u // 4, u % 4
-
-            at = rows(q * QR, QR)
-            pbuf[c, at, :] = pair_dot(TA, c, at).astype(BF16)
-            part_copy(u).start()
+        for group in runs(units):
+            take = by_piece if group[0] < 8 else by_position
+            base = len(sent)
+
+            def unit(k, u):
+                n = base + k
+                if base >= RING:
+                    part_copy(n - RING, u).wait_send()
+                pbuf[n % RING] = pair_dot(take, TA, u // 4, u % 4).astype(BF16)
+                part_copy(n, u).start()
+
+            if base < RING < base + len(group):
+                cut = RING - base
+                each(unit, group[:cut])
+                sent.extend(group[:cut])
+                base = len(sent)
+                each(unit, group[cut:])
+                sent.extend(group[cut:])
+            else:
+                each(unit, group)
+                sent.extend(group)
+
+    def spot(p):
+        pc, px, py = p % 2, (p // 2) % 4, p // 8
+        pa = px + pc * (py - px)
+        pb = py + pc * (px - py)
+        s = (pc + core) % 2
+        i = (pa - a + s * (a - b) + 4) % 4
+        j = (pb - b + s * (b - a) + 4) % 4
+        return (j + (j // 2) * (1 - 2 * (j % 2))) * 8 + s * 4 + i
+
+    spots = [spot(p) for p in range(32)]
+
+    def turn(load, q, start, count):
+        for k in range(0, count, 128):
+            size = min(128, count - k)
+            block = jnp.stack([load(r, k, size) for r in spots])
+            at = start + k if isinstance(start, int) else pl.multiple_of(start + k, 128)
+            out[rows(q * TR, TR), :, pl.ds(at, size)] = jnp.swapaxes(block, 0, 1).astype(BF16)
+
+    def final(*units):
+        for group in runs(units):
+            take = by_piece if group[0] < 8 else by_position
+
+            def unit(k, u):
+                c, q = u // 4, u % 4
+                facc[...] = pair_dot(take, TB, c, q)
+                part_copy(u, u).wait_recv()
+                total = facc[...] + inbuf[u].astype(F32)
+                if take is by_piece:
+                    inbuf[u] = total.astype(BF16)
+                else:
+                    facc[...] = total
+                    turn(lambda r, k, n: facc[rows(r * TR, TR), k : k + n], q, c * PC, PC)
+
+            each(unit, group)
+
+    def settle(c):
+        def step(q, carry):
+            def load(r, k, n):
+                return inbuf[c * 4 + r // 8, rows((r % 8) * T + q * TR, TR), k : k + n].astype(F32)
+
+            turn(load, q, c * PC, PC)
             return carry
 
-        each(unit, units)
-
-    def place(q, s):
-        j = q + (q // 2) * (1 - 2 * (q % 2))
-        spots = []
-        for i in range(4):
-            if s == 0:
-                spots.append(gid((a + i) % 4, (b + j) % 4, core))
-            else:
-                spots.append(gid((b + i) % 4, (a + j) % 4, 1 - core))
-        return spots
-
-    def out_wait(u):
-        c, q = u // 4, u % 4
-        ref = inbuf.at[c, rows(q * QR, QR)]
-        return pltpu.make_async_copy(ref, ref, out_sem.at[u])
-
-    def final(*units):
-        def unit(u, carry):
-            c, q = u // 4, u % 4
-
-            at = rows(q * QR, QR)
-            facc[...] = pair_dot(TB, c, at)
-            part_copy(u).wait_recv()
-            inbuf[c, at, :] = (facc[...] + inbuf[c, at, :].astype(F32)).astype(BF16)
-            for s in range(2):
-                for i, p in enumerate(place(q, s)):
-                    pltpu.make_async_copy(
-                        inbuf.at[c, rows((q * 8 + s * 4 + i) * T, T)],
-                        out_hbm.at[p, :, rows(c * PC, PC)],
-                        out_sem.at[u],
-                    ).start()
-            return carry
-
-        each(unit, units)
-
-    def last_a(r):
-        at = rows(r * QR, QR)
-        fF[at, :] = times(TB[own, at, :], wF[own]) + times(TC[zp % 2, at, :], wG[zp % 2])
-        fF[at, 0:PC] = fF[at, 0:PC] + times(TC[zo % 2, at, :], wG[zo % 2, 0:PC, :])
-
-    def last_b(r, carry):
-        at = rows(r * QR, QR)
-        fF[at, :] = fF[at, :] + times(TB[other, at, :], wF[other])
+        lax.fori_loop(0, 4, step, 0)
+
+    def last_a(q):
+        at = slice(q * QR, (q + 1) * QR)
+        most = times(by_piece(TB, own, q), wF[own]) + times(by_piece(TC, zp % 2, q), wG[zp % 2])
+        head = most[:, 0:PC] + times(by_piece(TC, zo % 2, q), wG[zo % 2, 0:PC, :])
+        fO[at, 0:PC] = head.astype(BF16)
+        fO[at, PC:] = most[:, PC:].astype(BF16)
+
+    def last_b(q, carry):
+        at = rows(q * QR, QR)
+        fO[at, :] = (fO[at, :].astype(F32) + times(by_piece(TB, other, q), wF[other])).astype(BF16)
         return carry
 
-    def last_c(r, carry):
-        at = rows(r * QR, QR)
-        fO[at, 0:PC] = fF[at, 0:PC].astype(BF16)
-        fO[at, PC:] = (fF[at, PC:] + times(TC[zo % 2, at, :], wG[zo % 2, PC:, :])).astype(BF16)
+    def last_c(q, carry):
+        facc[:, 0 : fO.shape[1] - PC] = times(by_position(TC, zo % 2, q), wG[zo % 2, PC:, :])
+
+        def load(r, k, n):
+            part = fO[rows(r * T + q * TR, TR), k : k + n].astype(F32)
+            return part if k < PC else part + facc[rows(r * TR, TR), k - PC : k - PC + n]
+
+        turn(load, q, NC * PC, fO.shape[1])
         return carry
 
     def forward_last(k):
@@ -327,99 +380,93 @@
     def send_across():
         remote(A.piece(0, 0), C.piece(0, 0), start_send.at[9], start_recv.at[9], dev_p)
 
-    def put_last():
-        for q in range(4):
-            for s in range(2):
-                for i, p in enumerate(place(q, s)):
-                    r = q * 8 + s * 4 + i
-                    pltpu.make_async_copy(
-                        fO.at[r * T : (r + 1) * T], out_hbm.at[p, :, NC * PC :], out_sem.at[4 * NC]
-                    ).start()
-
     normalise(0, TA, zp)
     A.e1()
     send_across()
     A.e3()
     A.e2()
+    normalise(1, TB, z)
     A.e4()
+    A.r(1)
     A.l(1)
-    normalise(1, TB, z)
+    own_cols(0)
+    A.l(3)
+    A.l(0)
     send_last()
-    own_cols(0)
+    A.e7(0)
+    partial(0)
+    B.e1()
+    A.l(2)
+    A.e7(2)
     A.r(0)
-    A.e7(0)
-    A.l(0)
-    A.r(3)
-    partial(0)
-    A.l(3)
-    A.l(2)
-    A.r(1)
-    B.e1()
-    A.e7(2)
     partial(2)
     A.r(2)
+    A.r(3)
     A.e7(1)
     partial(1)
-    A.o(3)
-    A.o(0)
+    B.e3()
+    A.o(1)
     own_cols(1)
     B.e2()
+    partial(6, 4, 5)
+    A.o(0)
+    A.o(3)
+    B.r(1)
+    A.o(2)
+    arrived(C.piece(0, 0), start_recv.at[9], dev_p)
+    B.e4()
     B.r(0)
-    B.e3()
-    partial(6, 4, 5)
-    arrived(C.piece(0, 0), start_recv.at[9], dev_p)
-    A.o(1)
-    B.e4()
     B.r(3)
+    A.e7(3)
+    own_cols(2)
+    B.l(0)
+    B.l(1)
+    partial(10, 9, 7)
+    B.l(3)
+    B.r(2)
+    B.l(2)
+    partial(3, 8, 11)
+    B.e7(0)
+    B.o(0)
     C.e1()
-    own_cols(2)
-    A.o(2)
-    B.e7(0)
-    A.e7(3)
-    partial(8, 11)
-    B.l(0)
-    B.l(3)
-    C.e3()
-    B.l(2)
-    B.l(1)
-    B.r(2)
-    B.r(1)
+    B.o(3)
+    B.e7(1)
     B.e7(2)
-    C.e2()
-    partial(3, 9, 7, 10)
-    B.e7(1)
-    B.o(3)
-    C.e4()
-    final(6, 1, 4, 5)
-    C.l(0)
-    B.o(0)
-    C.l(1)
-    final(8, 2, 0)
-    C.e7(0)
     B.o(2)
     B.o(1)
+    final(5, 0, 2, 4)
+    B.e7(3)
+    C.e2()
+    C.e3()
+    final(6, 10, 7, 1, 9, 3)
+    C.e4()
+    settle(0)
+    C.r(0)
+    C.r(3)
+    settle(1)
+    C.l(1)
+    own_cols(3)
+    C.e7(0)
+    partial(15, 13, 14)
+    C.r(1)
+    C.l(3)
+    C.r(2)
+    C.l(2)
+    C.l(0)
+    final(8, 11)
+    partial(12)
+    C.o(3)
+    C.e7(1)
     loads[2 + NC].wait()
     arrived(wG.at[zo % 2, 0:PC], w_recv.at[NC + 2], dev_w)
-    last_a(0)
-    C.r(1)
-    C.r(3)
-    own_cols(3)
-    partial(15, 13, 14, 12)
-    C.r(2)
-    C.l(2)
-    B.e7(3)
-    C.r(0)
-    C.l(3)
-    final(3, 9, 7, 11)
-    C.o(3)
-    C.o(0)
-    C.e7(1)
     last_a(1)
     C.o(1)
+    C.o(0)
+    C.o(2)
     C.e7(2)
     last_a(2)
-    C.o(2)
-    final(15, 10, 13)
+    last_a(0)
+    final(15, 13)
     C.e7(3)
     last_a(3)
     arrived(wF.at[other], w_recv.at[NC + 1], dev_w)
@@ -427,19 +474,16 @@
     final(14)
     arrived(wG.at[zo % 2, PC:], w_recv.at[NC + 3], dev_w)
     lax.fori_loop(0, 4, last_c, 0)
-    put_last()
     final(12)
 
     for copy in sends:
         copy.wait_send()
 
-    def drain(u, carry):
-        part_copy(u).wait_send()
-        out_wait(u).wait()
+    def drain(n, carry):
+        part_copy(n, n).wait_send()
         return carry
 
-    lax.fori_loop(0, 4 * NC, drain, 0)
-    pltpu.make_async_copy(fO, fO, out_sem.at[4 * NC]).wait()
+    lax.fori_loop(4 * NC - RING, 4 * NC, drain, 0)
 
 
 def body(tokens, norm_gain, joined_weight):
@@ -450,9 +494,9 @@
     dma = pltpu.SemaphoreType.DMA
     result = pl.pallas_call(
         kernel,
-        out_shape=jax.ShapeDtypeStruct((32, T, columns), BF16),
+        out_shape=pltpu.VMEM((T, 32, columns), BF16),
         in_specs=[any_space] * 3,
-        out_specs=any_space,
+        out_specs=pl.BlockSpec(memory_space=pltpu.VMEM),
         scratch_shapes=[
             pltpu.VMEM((count, depth), BF16),
             pltpu.VMEM((2 * T, depth), BF16),
@@ -460,16 +504,15 @@
             pltpu.VMEM((depth,), F32),
             pltpu.VMEM((4, 8, 128), F32),
             pltpu.VMEM((3, 2, 8, 128), F32),
-            pltpu.VMEM((2, ROWS, depth), BF16),
-            pltpu.VMEM((2, ROWS, depth), BF16),
-            pltpu.VMEM((2, ROWS, depth), BF16),
+            pltpu.VMEM((2, 32, T, depth), BF16),
+            pltpu.VMEM((2, 32, T, depth), BF16),
+            pltpu.VMEM((2, 32, T, depth), BF16),
             pltpu.VMEM((NC, 2, PC, depth), BF16),
             pltpu.VMEM((2, rest, depth), BF16),
             pltpu.VMEM((2, rest, depth), BF16),
-            pltpu.VMEM((NC, ROWS, PC), BF16),
-            pltpu.VMEM((NC, ROWS, PC), BF16),
+            pltpu.VMEM((RING, QR, PC), BF16),
+            pltpu.VMEM((4 * NC, QR, PC), BF16),
             pltpu.VMEM((QR, PC), F32),
-            pltpu.VMEM((ROWS, rest), F32),
             pltpu.VMEM((ROWS, rest), BF16),
             dma((3 + NC,)),
             dma((10,)),
@@ -480,13 +523,12 @@
             dma((4 * NC,)),
             dma((3 * 36,)),
             dma((3 * 32,)),
-            dma((4 * NC + 1,)),
         ],
         compiler_params=pltpu.CompilerParams(
-            collective_id=0, has_side_effects=True, vmem_limit_bytes=67_000_000
+            collective_id=0, has_side_effects=True, vmem_limit_bytes=LIMIT
         ),
     )(tokens, norm_gain, joined_weight.T)
-    return jnp.swapaxes(result, 0, 1)
+    return result
 
 
 def solution(mesh):

time: 143 us -> 138 us (0.965); the launches traced: 143 us -> 135 us
  local copies, waits for them, and re-layouts: 8.39 us -> 2.53 us
  Pallas kernels: 135 us -> 133 us
    transpose x1 -> x0, local copies, waits for them, and re-layouts: 8.39 us -> none  [body(): return jnp.swapaxes(result, 0, 1)]
    unnamed x0 -> x1, local copies, waits for them, and re-layouts: none -> 2.53 us
    pallas_call x1, Pallas kernels: 135 us -> 133 us  [body(): pl.pallas_call(kernel, out_shape=pltpu.VMEM((T, 32, columns), BF16), in_s...]
where the time goes in v4:
time: 138 us; the launch traced here: 135 us
  Pallas kernels  133 us (96%)
  local copies, waits for them, and re-layouts  2.53 us (2%)
    pallas_call x1, Pallas kernels, body(): pl.pallas_call(kernel, out_shape=pltpu.VMEM((T, 32, columns), BF16), in_s...  133 us

profile of v4, /device:TPU:0, one launch (start us, length us, event | category | flops | bytes accessed | tf_op | source)
XLA Modules:
  0.0 135.5 jit_solution(7462645072159810759)
XLA Ops:
  0.0 133.0 %shard_map.37 = bf16[64,32,1344]{2,1,0:T(8,128)(2,1)S(1)} custom-call(bf16[256,1536]{1,0:T(8,128)(2,1)} %tok_hbm.1, f32[1536]{0:T(1024)} %gain_hbm.1, bf16[1344,1536]{1,0:T(8,128)(2,1)} %bitcast.1), custom_call_target="tpu_custom_call" | custom-call | tf_op jit(solution)/shard_map/pallas_call | solution.py:495
  133.0 2.5 %copy.5 = bf16[64,32,1344]{2,1,0:T(8,128)(2,1)} copy(bf16[64,32,1344]{2,1,0:T(8,128)(2,1)S(1)} %shard_map.37) | data formatting | bytes 11010048

commit v5 on v4

--- a/solution.py
+++ b/solution.py
@@ -382,99 +382,103 @@
 
     normalise(0, TA, zp)
     A.e1()
+    A.e2()
+    A.e3()
+    A.e4()
     send_across()
-    A.e3()
-    A.e2()
     normalise(1, TB, z)
-    A.e4()
+    A.l(3)
+    A.r(0)
+    A.l(0)
+    own_cols(0)
+    A.e7(0)
+    A.r(3)
     A.r(1)
     A.l(1)
-    own_cols(0)
-    A.l(3)
-    A.l(0)
+    partial(0)
+    A.r(2)
+    A.l(2)
+    A.e7(1)
+    B.e1()
+    A.e7(2)
+    partial(2, 1)
+    own_cols(1)
+    A.o(1)
+    A.o(3)
     send_last()
-    A.e7(0)
-    partial(0)
-    B.e1()
-    A.l(2)
-    A.e7(2)
-    A.r(0)
-    partial(2)
-    A.r(2)
-    A.r(3)
-    A.e7(1)
-    partial(1)
+    A.o(2)
+    A.o(0)
+    B.e2()
+    partial(4, 6, 5)
     B.e3()
-    A.o(1)
-    own_cols(1)
-    B.e2()
-    partial(6, 4, 5)
-    A.o(0)
-    A.o(3)
+    B.e4()
+    B.l(0)
+    B.r(0)
+    arrived(C.piece(0, 0), start_recv.at[9], dev_p)
+    B.l(3)
+    B.r(3)
+    B.e7(0)
+    own_cols(2)
+    A.e7(3)
+    B.l(1)
     B.r(1)
-    A.o(2)
-    arrived(C.piece(0, 0), start_recv.at[9], dev_p)
-    B.e4()
-    B.r(0)
-    B.r(3)
-    A.e7(3)
-    own_cols(2)
-    B.l(0)
-    B.l(1)
-    partial(10, 9, 7)
-    B.l(3)
+    C.e1()
+    partial(10, 7, 3)
+    B.l(2)
+    final(4, 0)
     B.r(2)
-    B.l(2)
-    partial(3, 8, 11)
-    B.e7(0)
-    B.o(0)
-    C.e1()
-    B.o(3)
     B.e7(1)
-    B.e7(2)
-    B.o(2)
-    B.o(1)
-    final(5, 0, 2, 4)
-    B.e7(3)
     C.e2()
     C.e3()
-    final(6, 10, 7, 1, 9, 3)
+    final(1, 5)
+    partial(8)
+    B.o(3)
+    partial(11)
+    B.o(1)
     C.e4()
-    settle(0)
     C.r(0)
-    C.r(3)
-    settle(1)
-    C.l(1)
-    own_cols(3)
-    C.e7(0)
-    partial(15, 13, 14)
-    C.r(1)
-    C.l(3)
-    C.r(2)
-    C.l(2)
-    C.l(0)
-    final(8, 11)
-    partial(12)
-    C.o(3)
-    C.e7(1)
+    B.e7(2)
     loads[2 + NC].wait()
     arrived(wG.at[zo % 2, 0:PC], w_recv.at[NC + 2], dev_w)
+    B.o(0)
+    final(2, 6)
+    C.e7(0)
+    B.o(2)
+    partial(9)
+    last_a(0)
+    B.e7(3)
+    C.l(0)
+    C.l(3)
+    C.r(3)
+    final(10, 7, 8, 3)
+    C.r(1)
+    own_cols(3)
+    settle(0)
+    settle(1)
+    C.r(2)
+    C.l(1)
+    partial(15, 13, 12)
+    C.l(2)
+    C.o(3)
+    partial(14)
+    C.o(0)
+    final(9, 11)
+    C.o(2)
+    C.o(1)
+    C.e7(2)
+    C.e7(1)
     last_a(1)
-    C.o(1)
-    C.o(0)
-    C.o(2)
-    C.e7(2)
-    last_a(2)
-    last_a(0)
-    final(15, 13)
+    final(15)
     C.e7(3)
     last_a(3)
+    last_a(2)
+    final(13)
     arrived(wF.at[other], w_recv.at[NC + 1], dev_w)
     lax.fori_loop(0, 4, last_b, 0)
-    final(14)
+    final(12)
     arrived(wG.at[zo % 2, PC:], w_recv.at[NC + 3], dev_w)
     lax.fori_loop(0, 4, last_c, 0)
-    final(12)
+    final(14)
 
     for copy in sends:
         copy.wait_send()

time: 138 us -> 136 us (0.986); the launches traced: 135 us -> 136 us
  no operation moved by 1% of the time
where the time goes in v5:
time: 136 us
  Pallas kernels  134 us (99%)
  local copies, waits for them, and re-layouts  2.53 us (2%)
    pallas_call x1, Pallas kernels, body(): pl.pallas_call(kernel, out_shape=pltpu.VMEM((T, 32, columns), BF16), in_s...  134 us

profile of v5, /device:TPU:0, one launch (start us, length us, event | category | flops | bytes accessed | tf_op | source)
XLA Modules:
  0.0 136.2 jit_solution(10966898978970194023)
XLA Ops:
  0.0 133.7 %shard_map.37 = bf16[64,32,1344]{2,1,0:T(8,128)(2,1)S(1)} custom-call(bf16[256,1536]{1,0:T(8,128)(2,1)} %tok_hbm.1, f32[1536]{0:T(1024)} %gain_hbm.1, bf16[1344,1536]{1,0:T(8,128)(2,1)} %bitcast.1), custom_call_target="tpu_custom_call" | custom-call | tf_op jit(solution)/shard_map/pallas_call | solution.py:499
  133.7 2.5 %copy.5 = bf16[64,32,1344]{2,1,0:T(8,128)(2,1)} copy(bf16[64,32,1344]{2,1,0:T(8,128)(2,1)S(1)} %shard_map.37) | data formatting | bytes 11010048
